TPU v7x, 32 devices: a whole 2x2x4 slice. The times are simulated.
32 devices in a mesh: groups: 2 (over y), ep: 16 (over z, x, core).
Axes of the slice: x: 2, y: 2, z: 4, core: 2. Of those that a mesh axis runs over, the one named last changes fastest.
Arguments:
- tokens: bfloat16 [512, 2880], P(('groups', 'ep')), parts along dimension 0, may hold values from -6 to 6
- routes: int32 [512, 4], P(('groups', 'ep')), parts along dimension 0, may hold values from 0 to 7, all different within a row; in each aligned block of 16 rows (0 to 15, 16 to 31, ...) at most 16 rows name the same one
- gate_fixed: int32 [512, 4], P(('groups', 'ep')), parts along dimension 0, may hold values from 1 to 65535
- gate_weight: bfloat16 [16, 2880, 720], P('ep'), may hold values from -0.109375 to 0.109375
- up_weight: bfloat16 [16, 2880, 720], P('ep'), may hold values from -0.109375 to 0.109375
- down_weight: bfloat16 [16, 720, 2880], P('ep'), may hold values from -0.15625 to 0.15625
Outputs:
- mixed: bfloat16 [512, 2880], P(('groups', 'ep')), parts along dimension 0
There are 2 independent parts, one for each index of `groups`. A program takes and returns all parts, laid end to end along the dimension named above; an argument that names none is the same for every part. Nothing has to cross between parts.
Inputs may be any that keep to these rules, and one draw needn't show every extreme that they name: `routes`: each row names 4 different experts; the 16 rows of one device name any one expert at most 16 times.
All inputs are finite; a program needn't handle non-finite values.
Results may differ from a plain program's by a relative error of at most 0.0065.
Values may be sent and summed in bfloat16 or wider, within the bound.
No kernel may reach another device: no remote copies, remote signals or barrier semaphores. Data moves between devices by JAX's collectives and lax.ppermute only.
A program may use at most 64 MiB of HBM per device.

v0:
```python
import jax
import jax.numpy as jnp
from jax import lax
from jax.experimental import pallas as pl
from jax.experimental.pallas import tpu as pltpu
from jax.sharding import PartitionSpec as P


def swapped(value, axis, bit):
    mask = 2**bit
    pairs = [(source, source ^ mask) for source in range(lax.axis_size(axis))]
    return lax.ppermute(value, axis, pairs)


def turned(value, axis, step):
    size = lax.axis_size(axis)
    pairs = [(source, (source + 4 * step) % size) for source in range(size)]
    return lax.ppermute(value, axis, pairs)


def expert_half(expert_rows, w_gate, w_up, w_down):
    gate_part = jnp.dot(expert_rows, w_gate, preferred_element_type=jnp.float32)
    up_part = jnp.dot(expert_rows, w_up, preferred_element_type=jnp.float32)
    hidden = (jax.nn.silu(gate_part) * up_part).astype(jnp.bfloat16)
    return jnp.dot(hidden, w_down, preferred_element_type=jnp.float32).astype(jnp.bfloat16)


def slotted(tokens, routes, gate_fixed, gate_weight, up_weight, down_weight, capacity):
    devices_ep = lax.axis_size("ep")
    experts = devices_ep // 2
    tok_count = tokens.shape[0]
    top_count = routes.shape[1]
    width = tokens.shape[1]
    onehot = (routes[:, :, None] == jnp.arange(experts, dtype=jnp.int32)).astype(jnp.int32)
    flat_hot = onehot.reshape(tok_count * top_count, experts)
    before = jnp.cumsum(flat_hot, axis=0) - flat_hot
    position = jnp.sum(before * flat_hot, axis=1).reshape(tok_count, top_count)
    slot_index = routes * capacity + position
    select = (slot_index[:, :, None] == jnp.arange(experts * capacity, dtype=jnp.int32)).astype(
        jnp.int32
    )
    select = jnp.sum(select, axis=1).astype(jnp.bfloat16)
    packed = jnp.einsum("ts,td->sd", select, tokens, preferred_element_type=jnp.float32).astype(
        jnp.bfloat16
    )
    packed = packed.reshape(experts, 1, capacity, width)
    outgoing = jnp.broadcast_to(packed, (experts, 2, capacity, width)).reshape(
        devices_ep, capacity, width
    )
    received = lax.all_to_all(outgoing, "ep", split_axis=0, concat_axis=0, tiled=True)
    result = expert_half(received.reshape(-1, width), gate_weight[0], up_weight[0], down_weight[0])
    partial_value = result.reshape(received.shape[0], received.shape[1], width)
    parity = lax.axis_index("ep") % 2
    halves = partial_value.reshape(devices_ep, capacity, 2, width // 2)
    kept_half = lax.dynamic_index_in_dim(halves, parity, 2, keepdims=False)
    given_half = lax.dynamic_index_in_dim(halves, 1 - parity, 2, keepdims=False)
    partner = swapped(given_half, "ep", 0)
    reduced = (kept_half.astype(jnp.float32) + partner.astype(jnp.float32)).astype(jnp.bfloat16)
    returned = lax.all_to_all(reduced, "ep", split_axis=0, concat_axis=0, tiled=True)
    ordered = returned.reshape(experts, 2, capacity, width // 2).transpose(0, 2, 1, 3)
    expert_out = ordered.reshape(experts * capacity, width)
    picked = jnp.take(expert_out, slot_index.reshape(-1), axis=0).reshape(
        tok_count, top_count, width
    )
    weights = gate_fixed.astype(jnp.float32) / 65536.0
    mixed = jnp.sum(weights[:, :, None] * picked.astype(jnp.float32), axis=1)
    return mixed.astype(jnp.bfloat16)


def pack_tokens(tokens, routes, gate_fixed, experts):
    count, width = tokens.shape
    top = routes.shape[1]

    def kernel(tok_ref, route_ref, gate_ref, out_ref):
        rows = lax.broadcasted_iota(jnp.int32, (experts, count), 0)
        share = jnp.zeros((experts, count), jnp.float32)
        for k in range(top):
            value = gate_ref[k : k + 1, :].astype(jnp.float32) * (1.0 / 65536.0)
            share = share + jnp.where(route_ref[k : k + 1, :] == rows, value, 0.0)
        high = share.astype(jnp.bfloat16)
        low = (share - high.astype(jnp.float32)).astype(jnp.bfloat16)
        both = jnp.concatenate([high.astype(jnp.float32), low.astype(jnp.float32)], axis=0)
        unit = (
            lax.broadcasted_iota(jnp.int32, (count, count), 0)
            == lax.broadcasted_iota(jnp.int32, (count, count), 1)
        ).astype(jnp.bfloat16)
        columns = lax.dot_general(
            unit,
            both.astype(jnp.bfloat16),
            (((1,), (1,)), ((), ())),
            preferred_element_type=jnp.float32,
        )
        out_ref[:, :width] = tok_ref[...]
        out_ref[:, width:] = columns.astype(jnp.bfloat16)

    return pl.pallas_call(
        kernel,
        out_shape=jax.ShapeDtypeStruct((count, width + 2 * experts), jnp.bfloat16),
        in_specs=[pl.BlockSpec(memory_space=pltpu.VMEM)] * 3,
        out_specs=pl.BlockSpec(memory_space=pltpu.VMEM),
        compiler_params=pltpu.CompilerParams(vmem_limit_bytes=2 * 2**20),
        name="pack_tokens",
    )(tokens, routes.T, gate_fixed.T)


def fetched(weights):
    pieces = 3

    def kernel(*refs):
        number = len(weights)
        copies = []
        for n in range(number):
            rows = weights[n].shape[0] // pieces // 16 * 16
            for m in range(pieces):
                start = m * rows
                size = rows if m < pieces - 1 else weights[n].shape[0] - start
                copies.append(
                    pltpu.make_async_copy(
                        refs[n].at[pl.ds(start, size)],
                        refs[number + n].at[pl.ds(start, size)],
                        refs[2 * number].at[n * pieces + m],
                    )
                )
        for copy in copies:
            copy.start()
        for copy in copies:
            copy.wait()

    placed = [pltpu.with_memory_space_constraint(weight, pltpu.HBM) for weight in weights]
    return pl.pallas_call(
        kernel,
        out_shape=[pltpu.VMEM(weight.shape, weight.dtype) for weight in weights],
        in_specs=[pl.BlockSpec(memory_space=pl.ANY)] * len(weights),
        out_specs=[pl.BlockSpec(memory_space=pltpu.VMEM)] * len(weights),
        scratch_shapes=[pltpu.SemaphoreType.DMA((pieces * len(weights),))],
        compiler_params=pltpu.CompilerParams(vmem_limit_bytes=2**20),
        name="fetch",
    )(*placed)


def expert_chunks(chunks, expert, w_gate, w_up, w_down, width):
    count = chunks[0].shape[0]
    wide = chunks[0].shape[1]
    experts = (wide - width) // 2
    number = len(chunks)
    rows = number * count
    tail = width // 128 * 128
    step = 768

    def kernel(*refs):
        expert_ref = refs[0]
        in_refs = refs[1 : 1 + number]
        wg_ref, wu_ref, wd_ref = refs[1 + number : 4 + number]
        out_refs = refs[4 + number : 4 + 2 * number]
        x_ref = refs[4 + 2 * number]
        for n in range(number):
            x_ref[n * count : (n + 1) * count, :] = in_refs[n][...]
        lanes = lax.broadcasted_iota(jnp.int32, (8, wide - tail), 1) - (width - tail)
        mine = (lanes == expert_ref[0]) | (lanes == expert_ref[0] + experts)
        nt = (((1,), (1,)), ((), ()))
        share = lax.dot_general(
            jnp.where(mine, 1.0, 0.0).astype(jnp.bfloat16),
            x_ref[:, tail:],
            nt,
            preferred_element_type=jnp.float32,
        )[0:1, :]
        x = x_ref[:, :width]
        gate = lax.dot_general(wg_ref[...], x, nt, preferred_element_type=jnp.float32)
        up = lax.dot_general(wu_ref[...], x, nt, preferred_element_type=jnp.float32)
        hidden = gate / (1.0 + jnp.exp(-gate)) * up * share
        hidden = hidden.T.astype(jnp.bfloat16)
        for start in range(0, width, step):
            size = min(step, width - start)
            part = jnp.dot(
                hidden, wd_ref[:, start : start + size], preferred_element_type=jnp.float32
            ).astype(jnp.bfloat16)
            for m in range(number):
                out_refs[m][:, start : start + size] = part[m * count : (m + 1) * count, :]

    vmem = pl.BlockSpec(memory_space=pltpu.VMEM)
    return pl.pallas_call(
        kernel,
        out_shape=[jax.ShapeDtypeStruct((count, width), jnp.bfloat16)] * number,
        in_specs=[pl.BlockSpec(memory_space=pltpu.SMEM)] + [vmem] * (number + 3),
        out_specs=[vmem] * number,
        scratch_shapes=[pltpu.VMEM((rows, wide), jnp.bfloat16)],
        compiler_params=pltpu.CompilerParams(vmem_limit_bytes=16 * 2**20),
        name="expert_chunks",
    )(expert, *chunks, w_gate, w_up, w_down)


def added(*values):
    total = values[0].astype(jnp.float32)
    for value in values[1:]:
        total = total + value.astype(jnp.float32)
    return total.astype(jnp.bfloat16)


def dense(tokens, routes, gate_fixed, gate_weight, up_weight, down_weight):
    devices_ep = lax.axis_size("ep")
    layers = devices_ep // 4
    width = tokens.shape[1]
    expert = jnp.right_shift(lax.axis_index("ep").astype(jnp.int32), 1).reshape(1)
    tokens, expert = lax.optimization_barrier((tokens, expert))
    own = pack_tokens(tokens, routes, gate_fixed, devices_ep // 2)
    near = [own] + [turned(own, "ep", k) for k in range(1, layers)]
    far = [swapped(near[k], "ep", 1) for k in range(layers)]
    mine = near + far
    theirs = [swapped(mine[k], "ep", 0) for k in range(len(mine))]
    w_gate, w_up, w_down = fetched([gate_weight[0].T, up_weight[0].T, down_weight[0]])
    parts = expert_chunks(mine + theirs, expert, w_gate, w_up, w_down, width)
    kept, given = parts[: len(mine)], parts[len(mine) :]
    back = [swapped(given[k], "ep", 0) for k in range(len(given))]
    far_sums = [added(kept[layers + k], back[layers + k]) for k in range(layers)]
    from_far = [swapped(far_sums[k], "ep", 1) for k in range(layers)]
    near_sums = [added(kept[k], back[k], from_far[k]) for k in range(layers)]
    home = [turned(near_sums[k], "ep", -k) for k in range(1, layers)]
    return added(kept[0], back[0], from_far[0], *home)


def local(tokens, routes, gate_fixed, gate_weight, up_weight, down_weight):
    devices_ep = lax.axis_size("ep")
    tok_count, top_count = routes.shape
    capacity = min(tok_count, 2 * tok_count * top_count // (devices_ep // 2))
    if capacity == tok_count and devices_ep % 4 == 0:
        return dense(tokens, routes, gate_fixed, gate_weight, up_weight, down_weight)
    return slotted(tokens, routes, gate_fixed, gate_weight, up_weight, down_weight, capacity)


def solution(mesh):
    placed = (
        P(("groups", "ep"), None),
        P(("groups", "ep"), None),
        P(("groups", "ep"), None),
        P("ep", None, None),
        P("ep", None, None),
        P("ep", None, None),
    )
    return jax.shard_map(
        local, mesh=mesh, in_specs=placed, out_specs=P(("groups", "ep"), None), check_vma=False
    )
```

profile of v0, /device:TPU:0, one launch (start us, length us, event | category | flops | bytes accessed | tf_op | source)
XLA Modules:
  0.0 57.2 jit_solution(5536411672195154473)
XLA Ops:
  0.0 0.9 %copy-done = bf16[16,2880]{1,0:T(8,128)(2,1)S(1)} copy-done((bf16[16,2880]{1,0:T(8,128)(2,1)S(1)}, bf16[16,2880]{1,0:T(8,128)(2,1)}, u32[]{:S(2)}) %copy-start) | copy-done | bytes 92184
  0.9 0.7 %copy-done.1 = s32[16,4]{0,1:T(4,128)S(1)} copy-done((s32[16,4]{0,1:T(4,128)S(1)}, s32[16,4]{0,1:T(4,128)}, u32[]{:S(2)}) %copy-start.1) | copy-done | bytes 280
  1.6 0.7 %copy-done.2 = s32[16,4]{0,1:T(4,128)S(1)} copy-done((s32[16,4]{0,1:T(4,128)S(1)}, s32[16,4]{0,1:T(4,128)}, u32[]{:S(2)}) %copy-start.2) | copy-done | bytes 280
  2.3 0.2 pack_tokens.1.refs_1_
  2.5 3.0 %collective-permute-start.3 = (bf16[16,2896]{1,0:T(8,128)(2,1)S(1)}, bf16[16,2896]{1,0:T(8,128)(2,1)S(1)}, u32[]{:S(2)}, u32[]{:S(2)}) collective-permute-start(bf16[16,2896]{1,0:T(8,128)(2,1)S(1)} %pack_tokens.1.refs_1_), channel_id=1, source_target_pairs={{0,2},{1,3},{2,0},{3,1},{4,6},{5,7},{6,4},{7,5},{8,10},{9,11},{10,... | collective-permute-start | bytes 278024 | tf_op jit(solution)/shard_map/ppermute | solution.py:12
  5.4 3.6 %collective-permute-start.2 = (bf16[16,2896]{1,0:T(8,128)(2,1)S(1)}, bf16[16,2896]{1,0:T(8,128)(2,1)S(1)}, u32[]{:S(2)}, u32[]{:S(2)}) collective-permute-start(bf16[16,2896]{1,0:T(8,128)(2,1)S(1)} %pack_tokens.1.refs_1_), channel_id=1, source_target_pairs={{0,12},{1,13},{2,14},{3,15},{4,0},{5,1},{6,2},{7,3},{8,4},{9,5},{1... | collective-permute-start | bytes 278024 | tf_op jit(solution)/shard_map/ppermute | solution.py:18
  9.0 1.0 %collective-permute-start = (bf16[16,2896]{1,0:T(8,128)(2,1)S(1)}, bf16[16,2896]{1,0:T(8,128)(2,1)S(1)}, u32[]{:S(2)}, u32[]{:S(2)}) collective-permute-start(bf16[16,2896]{1,0:T(8,128)(2,1)S(1)} %pack_tokens.1.refs_1_), channel_id=1, source_target_pairs={{0,4},{1,5},{2,6},{3,7},{4,8},{5,9},{6,10},{7,11},{8,12},{9,13},{1... | collective-permute-start | bytes 278024 | tf_op jit(solution)/shard_map/ppermute | solution.py:18
  10.0 0.0 collective-permute-done.3.refs_5_
  10.0 0.0 collective-permute-start.11
  10.1 2.1 %collective-permute-done.2.refs_4_ = bf16[16,2896]{1,0:T(8,128)(2,1)S(1)} collective-permute-done((bf16[16,2896]{1,0:T(8,128)(2,1)S(1)}, bf16[16,2896]{1,0:T(8,128)(2,1)S(1)}, u32[]{:S(2)}, u32[]{:S(2)}) %collective-permute-start.2) | collective-permute-done | bytes 92704 | tf_op jit(solution)/shard_map/ppermute | solution.py:18
  12.1 0.0 collective-permute-start.10
  12.1 0.0 collective-permute-done.7.refs_9_
  12.1 0.5 collective-permute-start.6
  12.7 5.3 %collective-permute-done.1.refs_3_ = bf16[16,2896]{1,0:T(8,128)(2,1)S(1)} collective-permute-done((bf16[16,2896]{1,0:T(8,128)(2,1)S(1)}, bf16[16,2896]{1,0:T(8,128)(2,1)S(1)}, u32[]{:S(2)}, u32[]{:S(2)}) %collective-permute-start.1) | collective-permute-done | bytes 92704 | tf_op jit(solution)/shard_map/ppermute | solution.py:18
  18.0 0.5 collective-permute-start.5
  18.4 1.5 %collective-permute-start.4 = (bf16[16,2896]{1,0:T(8,128)(2,1)S(1)}, bf16[16,2896]{1,0:T(8,128)(2,1)S(1)}, u32[]{:S(2)}, u32[]{:S(2)}) collective-permute-start(bf16[16,2896]{1,0:T(8,128)(2,1)S(1)} %collective-permute-done.refs_2_), channel_id=1, source_target_pairs={{0,2},{1,3},{2,0},{3,1},{4,6},{5,7},{6,4},{7,5},{8,10},{9,11},{10,... | collective-permute-start | bytes 278024 | tf_op jit(solution)/shard_map/ppermute | solution.py:12
  20.0 0.5 collective-permute-start.8
  20.5 0.1 collective-permute-start.14
  20.6 3.0 %collective-permute-done.5.refs_7_ = bf16[16,2896]{1,0:T(8,128)(2,1)S(1)} collective-permute-done((bf16[16,2896]{1,0:T(8,128)(2,1)S(1)}, bf16[16,2896]{1,0:T(8,128)(2,1)S(1)}, u32[]{:S(2)}, u32[]{:S(2)}) %collective-permute-start.5) | collective-permute-done | bytes 92704 | tf_op jit(solution)/shard_map/ppermute | solution.py:12
  23.5 0.0 collective-permute-start.13
  23.5 1.2 %collective-permute-done.4.refs_6_ = bf16[16,2896]{1,0:T(8,128)(2,1)S(1)} collective-permute-done((bf16[16,2896]{1,0:T(8,128)(2,1)S(1)}, bf16[16,2896]{1,0:T(8,128)(2,1)S(1)}, u32[]{:S(2)}, u32[]{:S(2)}) %collective-permute-start.4) | collective-permute-done | bytes 92704 | tf_op jit(solution)/shard_map/ppermute | solution.py:12
  24.7 4.7 %fetch.1 = (bf16[720,2880]{1,0:T(8,128)(2,1)S(1)}, bf16[720,2880]{1,0:T(8,128)(2,1)S(1)}, bf16[720,2880]{1,0:T(8,128)(2,1)S(1)}) custom-call(bf16[720,2880]{1,0:T(8,128)(2,1)} %bitcast.12, bf16[720,2880]{1,0:T(8,128)(2,1)} %bitcast.13, bf16[720,2880]{1,0:T(8,128)(2,1)} %bitcast.14), custom_call_target="tpu_custom_call" | custom-call | tf_op jit(solution)/shard_map/fetch/pallas_call | solution.py:130
  29.4 0.0 collective-permute-done.9.refs_11_
  29.5 0.0 collective-permute-done.14.refs_16_
  29.5 3.9 %expert_chunks.1 = (bf16[16,2880]{1,0:T(8,128)(2,1)S(1)}, bf16[16,2880]{1,0:T(8,128)(2,1)S(1)}, bf16[16,2880]{1,0:T(8,128)(2,1)S(1)}, bf16[16,2880]{1,0:T(8,128)...) custom-call(s32[1]{0:T(128)} %bitcast.refs_0_, ...), custom_call_target="tpu_custom_call" | custom-call | tf_op jit(solution)/shard_map/expert_chunks/pallas_call | solution.py:181
  33.4 0.6 %collective-permute-start.16 = (bf16[16,2880]{1,0:T(8,128)(2,1)S(1)}, bf16[16,2880]{1,0:T(8,128)(2,1)S(1)}, u32[]{:S(2)}, u32[]{:S(2)}) collective-permute-start(bf16[16,2880]{1,0:T(8,128)(2,1)S(1)} %get-tuple-element.34), channel_id=1, source_target_pairs={{0,1},{1,0},{2,3},{3,2},{4,5},{5,4},{6,7},{7,6},{8,9},{9,8},{10,11... | collective-permute-start | bytes 276488 | tf_op jit(solution)/shard_map/ppermute | solution.py:12
  34.0 0.1 collective-permute-start.15
  34.1 0.4 collective-permute-start.18
  34.5 0.1 collective-permute-start.19
  34.6 0.4 collective-permute-start.22
  35.0 0.3 collective-permute-start.23
  35.3 0.5 collective-permute-done.19
  35.8 0.2 collective-permute-start.26
  36.0 0.3 collective-permute-done.23
  36.3 0.3 collective-permute-start.27
  36.6 1.0 %collective-permute-done.27 = bf16[16,2880]{1,0:T(8,128)(2,1)S(1)} collective-permute-done((bf16[16,2880]{1,0:T(8,128)(2,1)S(1)}, bf16[16,2880]{1,0:T(8,128)(2,1)S(1)}, u32[]{:S(2)}, u32[]{:S(2)}) %collective-permute-start.27) | collective-permute-done | bytes 92192 | tf_op jit(solution)/shard_map/ppermute | solution.py:12
  37.6 0.5 collective-permute-start.20
  38.1 1.6 %collective-permute-start.17 = (bf16[16,2880]{1,0:T(8,128)(2,1)S(1)}, bf16[16,2880]{1,0:T(8,128)(2,1)S(1)}, u32[]{:S(2)}, u32[]{:S(2)}) collective-permute-start(bf16[16,2880]{1,0:T(8,128)(2,1)S(1)} %add_convert_fusion.7), channel_id=1, source_target_pairs={{0,2},{1,3},{2,0},{3,1},{4,6},{5,7},{6,4},{7,5},{8,10},{9,11},{10,... | collective-permute-start | bytes 276488 | tf_op jit(solution)/shard_map/ppermute | solution.py:12
  39.7 3.4 %collective-permute-done.20 = bf16[16,2880]{1,0:T(8,128)(2,1)S(1)} collective-permute-done((bf16[16,2880]{1,0:T(8,128)(2,1)S(1)}, bf16[16,2880]{1,0:T(8,128)(2,1)S(1)}, u32[]{:S(2)}, u32[]{:S(2)}) %collective-permute-start.20) | collective-permute-done | bytes 92192 | tf_op jit(solution)/shard_map/ppermute | solution.py:12
  43.2 0.4 collective-permute-start.24
  43.6 1.7 %collective-permute-start.28 = (bf16[16,2880]{1,0:T(8,128)(2,1)S(1)}, bf16[16,2880]{1,0:T(8,128)(2,1)S(1)}, u32[]{:S(2)}, u32[]{:S(2)}) collective-permute-start(bf16[16,2880]{1,0:T(8,128)(2,1)S(1)} %add_convert_fusion.2), channel_id=1, source_target_pairs={{0,2},{1,3},{2,0},{3,1},{4,6},{5,7},{6,4},{7,5},{8,10},{9,11},{10,... | collective-permute-start | bytes 276488 | tf_op jit(solution)/shard_map/ppermute | solution.py:12
  45.3 2.4 %collective-permute-done.24 = bf16[16,2880]{1,0:T(8,128)(2,1)S(1)} collective-permute-done((bf16[16,2880]{1,0:T(8,128)(2,1)S(1)}, bf16[16,2880]{1,0:T(8,128)(2,1)S(1)}, u32[]{:S(2)}, u32[]{:S(2)}) %collective-permute-start.24) | collective-permute-done | bytes 92192 | tf_op jit(solution)/shard_map/ppermute | solution.py:12
  47.7 1.0 %collective-permute-start.21 = (bf16[16,2880]{1,0:T(8,128)(2,1)S(1)}, bf16[16,2880]{1,0:T(8,128)(2,1)S(1)}, u32[]{:S(2)}, u32[]{:S(2)}) collective-permute-start(bf16[16,2880]{1,0:T(8,128)(2,1)S(1)} %add_convert_fusion.5), channel_id=1, source_target_pairs={{0,12},{1,13},{2,14},{3,15},{4,0},{5,1},{6,2},{7,3},{8,4},{9,5},{1... | collective-permute-start | bytes 276488 | tf_op jit(solution)/shard_map/ppermute | solution.py:18
  48.8 0.1 collective-permute-start.25
  49.0 1.2 %collective-permute-start.29 = (bf16[16,2880]{1,0:T(8,128)(2,1)S(1)}, bf16[16,2880]{1,0:T(8,128)(2,1)S(1)}, u32[]{:S(2)}, u32[]{:S(2)}) collective-permute-start(bf16[16,2880]{1,0:T(8,128)(2,1)S(1)} %add_convert_fusion.1), channel_id=1, source_target_pairs={{0,4},{1,5},{2,6},{3,7},{4,8},{5,9},{6,10},{7,11},{8,12},{9,13},{1... | collective-permute-start | bytes 276488 | tf_op jit(solution)/shard_map/ppermute | solution.py:18
  50.1 4.3 %collective-permute-done.21 = bf16[16,2880]{1,0:T(8,128)(2,1)S(1)} collective-permute-done((bf16[16,2880]{1,0:T(8,128)(2,1)S(1)}, bf16[16,2880]{1,0:T(8,128)(2,1)S(1)}, u32[]{:S(2)}, u32[]{:S(2)}) %collective-permute-start.21) | collective-permute-done | bytes 92192 | tf_op jit(solution)/shard_map/ppermute | solution.py:18
  54.5 2.0 %collective-permute-done.25 = bf16[16,2880]{1,0:T(8,128)(2,1)S(1)} collective-permute-done((bf16[16,2880]{1,0:T(8,128)(2,1)S(1)}, bf16[16,2880]{1,0:T(8,128)(2,1)S(1)}, u32[]{:S(2)}, u32[]{:S(2)}) %collective-permute-start.25) | collective-permute-done | bytes 92192 | tf_op jit(solution)/shard_map/ppermute | solution.py:18
  56.5 0.7 %add_convert_fusion = bf16[16,2880]{1,0:T(8,128)(2,1)} fusion(bf16[16,2880]{1,0:T(8,128)(2,1)S(1)} %collective-permute-done.29, bf16[16,2880]{1,0:T(8,128)(2,1)S(1)} %collective-permute-done.25, bf16[16,2880]{1,0:T(8,128)(2,1)S(1)} %collective-permute-done.21, bf16[16,2880]{1,0:T(8,128)(2,1)S(1)} %collective-permute-done.17, ...), kind=kLoop, calls=%fused_computation | loop fusion | flops 552960 | bytes 645120 | tf_op jit(solution)/shard_map/convert_element_type | solution.py:196
  (29 shorter events, 0.3 us)
Async XLA Ops:
  0.0 0.9 %copy-start = (bf16[16,2880]{1,0:T(8,128)(2,1)S(1)}, bf16[16,2880]{1,0:T(8,128)(2,1)}, u32[]{:S(2)}) copy-start(bf16[16,2880]{1,0:T(8,128)(2,1)} %tok_ref) | copy-start | bytes 276484
  0.9 0.7 %copy-start.1 = (s32[16,4]{0,1:T(4,128)S(1)}, s32[16,4]{0,1:T(4,128)}, u32[]{:S(2)}) copy-start(s32[16,4]{0,1:T(4,128)} %param.7) | copy-start | bytes 772
  1.6 0.7 %copy-start.2 = (s32[16,4]{0,1:T(4,128)S(1)}, s32[16,4]{0,1:T(4,128)}, u32[]{:S(2)}) copy-start(s32[16,4]{0,1:T(4,128)} %param.8) | copy-start | bytes 772
  2.5 7.6 %collective-permute-start.3 = (bf16[16,2896]{1,0:T(8,128)(2,1)S(1)}, bf16[16,2896]{1,0:T(8,128)(2,1)S(1)}, u32[]{:S(2)}, u32[]{:S(2)}) collective-permute-start(bf16[16,2896]{1,0:T(8,128)(2,1)S(1)} %pack_tokens.1.refs_1_), channel_id=1, source_target_pairs={{0,2},{1,3},{2,0},{3,1},{4,6},{5,7},{6,4},{7,5},{8,10},{9,11},{10,... | collective-permute-start | bytes 278024 | tf_op jit(solution)/shard_map/ppermute | solution.py:12
  5.4 6.7 %collective-permute-start.2 = (bf16[16,2896]{1,0:T(8,128)(2,1)S(1)}, bf16[16,2896]{1,0:T(8,128)(2,1)S(1)}, u32[]{:S(2)}, u32[]{:S(2)}) collective-permute-start(bf16[16,2896]{1,0:T(8,128)(2,1)S(1)} %pack_tokens.1.refs_1_), channel_id=1, source_target_pairs={{0,12},{1,13},{2,14},{3,15},{4,0},{5,1},{6,2},{7,3},{8,4},{9,5},{1... | collective-permute-start | bytes 278024 | tf_op jit(solution)/shard_map/ppermute | solution.py:18
  9.0 3.1 %collective-permute-start.7 = (bf16[16,2896]{1,0:T(8,128)(2,1)S(1)}, bf16[16,2896]{1,0:T(8,128)(2,1)S(1)}, u32[]{:S(2)}, u32[]{:S(2)}) collective-permute-start(bf16[16,2896]{1,0:T(8,128)(2,1)S(1)} %pack_tokens.1.refs_1_), channel_id=1, source_target_pairs={{0,1},{1,0},{2,3},{3,2},{4,5},{5,4},{6,7},{7,6},{8,9},{9,8},{10,11... | collective-permute-start | bytes 278024 | tf_op jit(solution)/shard_map/ppermute | solution.py:12
  9.0 8.9 %collective-permute-start.1 = (bf16[16,2896]{1,0:T(8,128)(2,1)S(1)}, bf16[16,2896]{1,0:T(8,128)(2,1)S(1)}, u32[]{:S(2)}, u32[]{:S(2)}) collective-permute-start(bf16[16,2896]{1,0:T(8,128)(2,1)S(1)} %pack_tokens.1.refs_1_), channel_id=1, source_target_pairs={{0,8},{1,9},{2,10},{3,11},{4,12},{5,13},{6,14},{7,15},{8,0},{9,1},... | collective-permute-start | bytes 278024 | tf_op jit(solution)/shard_map/ppermute | solution.py:18
  9.0 9.4 %collective-permute-start = (bf16[16,2896]{1,0:T(8,128)(2,1)S(1)}, bf16[16,2896]{1,0:T(8,128)(2,1)S(1)}, u32[]{:S(2)}, u32[]{:S(2)}) collective-permute-start(bf16[16,2896]{1,0:T(8,128)(2,1)S(1)} %pack_tokens.1.refs_1_), channel_id=1, source_target_pairs={{0,4},{1,5},{2,6},{3,7},{4,8},{5,9},{6,10},{7,11},{8,12},{9,13},{1... | collective-permute-start | bytes 278024 | tf_op jit(solution)/shard_map/ppermute | solution.py:18
  10.0 9.9 %collective-permute-start.11 = (bf16[16,2896]{1,0:T(8,128)(2,1)S(1)}, bf16[16,2896]{1,0:T(8,128)(2,1)S(1)}, u32[]{:S(2)}, u32[]{:S(2)}) collective-permute-start(bf16[16,2896]{1,0:T(8,128)(2,1)S(1)} %collective-permute-done.3.refs_5_), channel_id=1, source_target_pairs={{0,1},{1,0},{2,3},{3,2},{4,5},{5,4},{6,7},{7,6},{8,9},{9,8},{10,11... | collective-permute-start | bytes 278024 | tf_op jit(solution)/shard_map/ppermute | solution.py:12
  12.1 7.9 %collective-permute-start.10 = (bf16[16,2896]{1,0:T(8,128)(2,1)S(1)}, bf16[16,2896]{1,0:T(8,128)(2,1)S(1)}, u32[]{:S(2)}, u32[]{:S(2)}) collective-permute-start(bf16[16,2896]{1,0:T(8,128)(2,1)S(1)} %collective-permute-done.2.refs_4_), channel_id=1, source_target_pairs={{0,1},{1,0},{2,3},{3,2},{4,5},{5,4},{6,7},{7,6},{8,9},{9,8},{10,11... | collective-permute-start | bytes 278024 | tf_op jit(solution)/shard_map/ppermute | solution.py:12
  12.1 8.4 %collective-permute-start.6 = (bf16[16,2896]{1,0:T(8,128)(2,1)S(1)}, bf16[16,2896]{1,0:T(8,128)(2,1)S(1)}, u32[]{:S(2)}, u32[]{:S(2)}) collective-permute-start(bf16[16,2896]{1,0:T(8,128)(2,1)S(1)} %collective-permute-done.2.refs_4_), channel_id=1, source_target_pairs={{0,2},{1,3},{2,0},{3,1},{4,6},{5,7},{6,4},{7,5},{8,10},{9,11},{10,... | collective-permute-start | bytes 278024 | tf_op jit(solution)/shard_map/ppermute | solution.py:12
  18.0 5.6 %collective-permute-start.5 = (bf16[16,2896]{1,0:T(8,128)(2,1)S(1)}, bf16[16,2896]{1,0:T(8,128)(2,1)S(1)}, u32[]{:S(2)}, u32[]{:S(2)}) collective-permute-start(bf16[16,2896]{1,0:T(8,128)(2,1)S(1)} %collective-permute-done.1.refs_3_), channel_id=1, source_target_pairs={{0,2},{1,3},{2,0},{3,1},{4,6},{5,7},{6,4},{7,5},{8,10},{9,11},{10,... | collective-permute-start | bytes 278024 | tf_op jit(solution)/shard_map/ppermute | solution.py:12
  18.4 6.3 %collective-permute-start.4 = (bf16[16,2896]{1,0:T(8,128)(2,1)S(1)}, bf16[16,2896]{1,0:T(8,128)(2,1)S(1)}, u32[]{:S(2)}, u32[]{:S(2)}) collective-permute-start(bf16[16,2896]{1,0:T(8,128)(2,1)S(1)} %collective-permute-done.refs_2_), channel_id=1, source_target_pairs={{0,2},{1,3},{2,0},{3,1},{4,6},{5,7},{6,4},{7,5},{8,10},{9,11},{10,... | collective-permute-start | bytes 278024 | tf_op jit(solution)/shard_map/ppermute | solution.py:12
  20.0 9.5 %collective-permute-start.9 = (bf16[16,2896]{1,0:T(8,128)(2,1)S(1)}, bf16[16,2896]{1,0:T(8,128)(2,1)S(1)}, u32[]{:S(2)}, u32[]{:S(2)}) collective-permute-start(bf16[16,2896]{1,0:T(8,128)(2,1)S(1)} %collective-permute-done.1.refs_3_), channel_id=1, source_target_pairs={{0,1},{1,0},{2,3},{3,2},{4,5},{5,4},{6,7},{7,6},{8,9},{9,8},{10,11... | collective-permute-start | bytes 278024 | tf_op jit(solution)/shard_map/ppermute | solution.py:12
  20.0 9.5 %collective-permute-start.8 = (bf16[16,2896]{1,0:T(8,128)(2,1)S(1)}, bf16[16,2896]{1,0:T(8,128)(2,1)S(1)}, u32[]{:S(2)}, u32[]{:S(2)}) collective-permute-start(bf16[16,2896]{1,0:T(8,128)(2,1)S(1)} %collective-permute-done.refs_2_), channel_id=1, source_target_pairs={{0,1},{1,0},{2,3},{3,2},{4,5},{5,4},{6,7},{7,6},{8,9},{9,8},{10,11... | collective-permute-start | bytes 278024 | tf_op jit(solution)/shard_map/ppermute | solution.py:12
  20.5 9.0 %collective-permute-start.14 = (bf16[16,2896]{1,0:T(8,128)(2,1)S(1)}, bf16[16,2896]{1,0:T(8,128)(2,1)S(1)}, u32[]{:S(2)}, u32[]{:S(2)}) collective-permute-start(bf16[16,2896]{1,0:T(8,128)(2,1)S(1)} %collective-permute-done.6.refs_8_), channel_id=1, source_target_pairs={{0,1},{1,0},{2,3},{3,2},{4,5},{5,4},{6,7},{7,6},{8,9},{9,8},{10,11... | collective-permute-start | bytes 278024 | tf_op jit(solution)/shard_map/ppermute | solution.py:12
  23.5 5.9 %collective-permute-start.13 = (bf16[16,2896]{1,0:T(8,128)(2,1)S(1)}, bf16[16,2896]{1,0:T(8,128)(2,1)S(1)}, u32[]{:S(2)}, u32[]{:S(2)}) collective-permute-start(bf16[16,2896]{1,0:T(8,128)(2,1)S(1)} %collective-permute-done.5.refs_7_), channel_id=1, source_target_pairs={{0,1},{1,0},{2,3},{3,2},{4,5},{5,4},{6,7},{7,6},{8,9},{9,8},{10,11... | collective-permute-start | bytes 278024 | tf_op jit(solution)/shard_map/ppermute | solution.py:12
  24.7 4.8 %collective-permute-start.12 = (bf16[16,2896]{1,0:T(8,128)(2,1)S(1)}, bf16[16,2896]{1,0:T(8,128)(2,1)S(1)}, u32[]{:S(2)}, u32[]{:S(2)}) collective-permute-start(bf16[16,2896]{1,0:T(8,128)(2,1)S(1)} %collective-permute-done.4.refs_6_), channel_id=1, source_target_pairs={{0,1},{1,0},{2,3},{3,2},{4,5},{5,4},{6,7},{7,6},{8,9},{9,8},{10,11... | collective-permute-start | bytes 278024 | tf_op jit(solution)/shard_map/ppermute | solution.py:12
  33.4 1.6 %collective-permute-start.16 = (bf16[16,2880]{1,0:T(8,128)(2,1)S(1)}, bf16[16,2880]{1,0:T(8,128)(2,1)S(1)}, u32[]{:S(2)}, u32[]{:S(2)}) collective-permute-start(bf16[16,2880]{1,0:T(8,128)(2,1)S(1)} %get-tuple-element.34), channel_id=1, source_target_pairs={{0,1},{1,0},{2,3},{3,2},{4,5},{5,4},{6,7},{7,6},{8,9},{9,8},{10,11... | collective-permute-start | bytes 276488 | tf_op jit(solution)/shard_map/ppermute | solution.py:12
  34.0 16.1 %collective-permute-start.15 = (bf16[16,2880]{1,0:T(8,128)(2,1)S(1)}, bf16[16,2880]{1,0:T(8,128)(2,1)S(1)}, u32[]{:S(2)}, u32[]{:S(2)}) collective-permute-start(bf16[16,2880]{1,0:T(8,128)(2,1)S(1)} %get-tuple-element.32), channel_id=1, source_target_pairs={{0,1},{1,0},{2,3},{3,2},{4,5},{5,4},{6,7},{7,6},{8,9},{9,8},{10,11... | collective-permute-start | bytes 276488 | tf_op jit(solution)/shard_map/ppermute | solution.py:12
  34.1 4.0 %collective-permute-start.18 = (bf16[16,2880]{1,0:T(8,128)(2,1)S(1)}, bf16[16,2880]{1,0:T(8,128)(2,1)S(1)}, u32[]{:S(2)}, u32[]{:S(2)}) collective-permute-start(bf16[16,2880]{1,0:T(8,128)(2,1)S(1)} %get-tuple-element.36), channel_id=1, source_target_pairs={{0,1},{1,0},{2,3},{3,2},{4,5},{5,4},{6,7},{7,6},{8,9},{9,8},{10,11... | collective-permute-start | bytes 276488 | tf_op jit(solution)/shard_map/ppermute | solution.py:12
  34.5 1.3 %collective-permute-start.19 = (bf16[16,2880]{1,0:T(8,128)(2,1)S(1)}, bf16[16,2880]{1,0:T(8,128)(2,1)S(1)}, u32[]{:S(2)}, u32[]{:S(2)}) collective-permute-start(bf16[16,2880]{1,0:T(8,128)(2,1)S(1)} %get-tuple-element.38), channel_id=1, source_target_pairs={{0,1},{1,0},{2,3},{3,2},{4,5},{5,4},{6,7},{7,6},{8,9},{9,8},{10,11... | collective-permute-start | bytes 276488 | tf_op jit(solution)/shard_map/ppermute | solution.py:12
  34.6 9.1 %collective-permute-start.22 = (bf16[16,2880]{1,0:T(8,128)(2,1)S(1)}, bf16[16,2880]{1,0:T(8,128)(2,1)S(1)}, u32[]{:S(2)}, u32[]{:S(2)}) collective-permute-start(bf16[16,2880]{1,0:T(8,128)(2,1)S(1)} %get-tuple-element.40), channel_id=1, source_target_pairs={{0,1},{1,0},{2,3},{3,2},{4,5},{5,4},{6,7},{7,6},{8,9},{9,8},{10,11... | collective-permute-start | bytes 276488 | tf_op jit(solution)/shard_map/ppermute | solution.py:12
  35.0 1.3 %collective-permute-start.23 = (bf16[16,2880]{1,0:T(8,128)(2,1)S(1)}, bf16[16,2880]{1,0:T(8,128)(2,1)S(1)}, u32[]{:S(2)}, u32[]{:S(2)}) collective-permute-start(bf16[16,2880]{1,0:T(8,128)(2,1)S(1)} %get-tuple-element.42), channel_id=1, source_target_pairs={{0,1},{1,0},{2,3},{3,2},{4,5},{5,4},{6,7},{7,6},{8,9},{9,8},{10,11... | collective-permute-start | bytes 276488 | tf_op jit(solution)/shard_map/ppermute | solution.py:12
  35.8 13.0 %collective-permute-start.26 = (bf16[16,2880]{1,0:T(8,128)(2,1)S(1)}, bf16[16,2880]{1,0:T(8,128)(2,1)S(1)}, u32[]{:S(2)}, u32[]{:S(2)}) collective-permute-start(bf16[16,2880]{1,0:T(8,128)(2,1)S(1)} %get-tuple-element.44), channel_id=1, source_target_pairs={{0,1},{1,0},{2,3},{3,2},{4,5},{5,4},{6,7},{7,6},{8,9},{9,8},{10,11... | collective-permute-start | bytes 276488 | tf_op jit(solution)/shard_map/ppermute | solution.py:12
  36.3 1.3 %collective-permute-start.27 = (bf16[16,2880]{1,0:T(8,128)(2,1)S(1)}, bf16[16,2880]{1,0:T(8,128)(2,1)S(1)}, u32[]{:S(2)}, u32[]{:S(2)}) collective-permute-start(bf16[16,2880]{1,0:T(8,128)(2,1)S(1)} %get-tuple-element.46), channel_id=1, source_target_pairs={{0,1},{1,0},{2,3},{3,2},{4,5},{5,4},{6,7},{7,6},{8,9},{9,8},{10,11... | collective-permute-start | bytes 276488 | tf_op jit(solution)/shard_map/ppermute | solution.py:12
  37.6 5.6 %collective-permute-start.20 = (bf16[16,2880]{1,0:T(8,128)(2,1)S(1)}, bf16[16,2880]{1,0:T(8,128)(2,1)S(1)}, u32[]{:S(2)}, u32[]{:S(2)}) collective-permute-start(bf16[16,2880]{1,0:T(8,128)(2,1)S(1)} %add_convert_fusion.6), channel_id=1, source_target_pairs={{0,2},{1,3},{2,0},{3,1},{4,6},{5,7},{6,4},{7,5},{8,10},{9,11},{10,... | collective-permute-start | bytes 276488 | tf_op jit(solution)/shard_map/ppermute | solution.py:12
  38.1 12.0 %collective-permute-start.17 = (bf16[16,2880]{1,0:T(8,128)(2,1)S(1)}, bf16[16,2880]{1,0:T(8,128)(2,1)S(1)}, u32[]{:S(2)}, u32[]{:S(2)}) collective-permute-start(bf16[16,2880]{1,0:T(8,128)(2,1)S(1)} %add_convert_fusion.7), channel_id=1, source_target_pairs={{0,2},{1,3},{2,0},{3,1},{4,6},{5,7},{6,4},{7,5},{8,10},{9,11},{10,... | collective-permute-start | bytes 276488 | tf_op jit(solution)/shard_map/ppermute | solution.py:12
  43.2 4.6 %collective-permute-start.24 = (bf16[16,2880]{1,0:T(8,128)(2,1)S(1)}, bf16[16,2880]{1,0:T(8,128)(2,1)S(1)}, u32[]{:S(2)}, u32[]{:S(2)}) collective-permute-start(bf16[16,2880]{1,0:T(8,128)(2,1)S(1)} %add_convert_fusion.4), channel_id=1, source_target_pairs={{0,2},{1,3},{2,0},{3,1},{4,6},{5,7},{6,4},{7,5},{8,10},{9,11},{10,... | collective-permute-start | bytes 276488 | tf_op jit(solution)/shard_map/ppermute | solution.py:12
  43.6 5.3 %collective-permute-start.28 = (bf16[16,2880]{1,0:T(8,128)(2,1)S(1)}, bf16[16,2880]{1,0:T(8,128)(2,1)S(1)}, u32[]{:S(2)}, u32[]{:S(2)}) collective-permute-start(bf16[16,2880]{1,0:T(8,128)(2,1)S(1)} %add_convert_fusion.2), channel_id=1, source_target_pairs={{0,2},{1,3},{2,0},{3,1},{4,6},{5,7},{6,4},{7,5},{8,10},{9,11},{10,... | collective-permute-start | bytes 276488 | tf_op jit(solution)/shard_map/ppermute | solution.py:12
  47.7 6.7 %collective-permute-start.21 = (bf16[16,2880]{1,0:T(8,128)(2,1)S(1)}, bf16[16,2880]{1,0:T(8,128)(2,1)S(1)}, u32[]{:S(2)}, u32[]{:S(2)}) collective-permute-start(bf16[16,2880]{1,0:T(8,128)(2,1)S(1)} %add_convert_fusion.5), channel_id=1, source_target_pairs={{0,12},{1,13},{2,14},{3,15},{4,0},{5,1},{6,2},{7,3},{8,4},{9,5},{1... | collective-permute-start | bytes 276488 | tf_op jit(solution)/shard_map/ppermute | solution.py:18
  48.8 7.7 %collective-permute-start.25 = (bf16[16,2880]{1,0:T(8,128)(2,1)S(1)}, bf16[16,2880]{1,0:T(8,128)(2,1)S(1)}, u32[]{:S(2)}, u32[]{:S(2)}) collective-permute-start(bf16[16,2880]{1,0:T(8,128)(2,1)S(1)} %add_convert_fusion.3), channel_id=1, source_target_pairs={{0,8},{1,9},{2,10},{3,11},{4,12},{5,13},{6,14},{7,15},{8,0},{9,1},... | collective-permute-start | bytes 276488 | tf_op jit(solution)/shard_map/ppermute | solution.py:18
  49.0 7.5 %collective-permute-start.29 = (bf16[16,2880]{1,0:T(8,128)(2,1)S(1)}, bf16[16,2880]{1,0:T(8,128)(2,1)S(1)}, u32[]{:S(2)}, u32[]{:S(2)}) collective-permute-start(bf16[16,2880]{1,0:T(8,128)(2,1)S(1)} %add_convert_fusion.1), channel_id=1, source_target_pairs={{0,4},{1,5},{2,6},{3,7},{4,8},{5,9},{6,10},{7,11},{8,12},{9,13},{1... | collective-permute-start | bytes 276488 | tf_op jit(solution)/shard_map/ppermute | solution.py:18
where the time goes:
time: 57.4 us; the launch traced here: 57.2 us
  waiting for transfers between devices  25.6 us (45%)
  starting transfers between devices  19.5 us (34%)
  Pallas kernels  8.83 us (15%)
  local copies, waits for them, and re-layouts  2.25 us (4%)
  other arithmetic  0.95 us (2%)
    ppermute x6, waiting for transfers between devices, turned(): return lax.ppermute(value, axis, pairs)  13.7 us
    ppermute x24, starting transfers between devices, swapped(): return lax.ppermute(value, axis, pairs)  12.6 us
    ppermute x24, waiting for transfers between devices, swapped(): return lax.ppermute(value, axis, pairs)  11.8 us
    ppermute x6, starting transfers between devices, turned(): return lax.ppermute(value, axis, pairs)  6.87 us
    pallas_call x1, Pallas kernels, fetched(): pl.pallas_call(kernel, out_shape=[pltpu.VMEM(weight.shape, weight.dtype)...  4.73 us
    pallas_call x1, Pallas kernels, expert_chunks(): pl.pallas_call(kernel, out_shape=[jax.ShapeDtypeStruct((count, width), jn...  3.9 us
    unnamed x6, local copies, waits for them, and re-layouts  2.25 us
  transfers between devices with their start and end apart: 30, of which 11 were waited for; matrix products, arithmetic and copies ran while one was open for 0% of the time, Pallas kernels for 8%

commit v1 on v0

--- a/solution.py
+++ b/solution.py
@@ -12,9 +12,8 @@
     return lax.ppermute(value, axis, pairs)
 
 
-def turned(value, axis, step):
-    size = lax.axis_size(axis)
-    pairs = [(source, (source + 4 * step) % size) for source in range(size)]
+def moved(value, axis, mask):
+    pairs = [(source, source ^ mask) for source in range(lax.axis_size(axis))]
     return lax.ppermute(value, axis, pairs)
 
 
@@ -71,7 +70,17 @@
     count, width = tokens.shape
     top = routes.shape[1]
 
-    def kernel(tok_ref, route_ref, gate_ref, out_ref):
+    def kernel(tok_hbm, route_hbm, gate_hbm, out_ref, tok_ref, route_ref, gate_ref, sem):
+        copies = [
+            pltpu.make_async_copy(source, place, sem.at[n])
+            for n, (source, place) in enumerate(
+                ((tok_hbm, tok_ref), (route_hbm, route_ref), (gate_hbm, gate_ref))
+            )
+        ]
+        for copy in copies:
+            copy.start()
+        copies[1].wait()
+        copies[2].wait()
         rows = lax.broadcasted_iota(jnp.int32, (experts, count), 0)
         share = jnp.zeros((experts, count), jnp.float32)
         for k in range(top):
@@ -90,21 +99,28 @@
             (((1,), (1,)), ((), ())),
             preferred_element_type=jnp.float32,
         )
+        copies[0].wait()
         out_ref[:, :width] = tok_ref[...]
         out_ref[:, width:] = columns.astype(jnp.bfloat16)
 
+    given = [
+        pltpu.with_memory_space_constraint(value, pltpu.HBM)
+        for value in (tokens, routes.T, gate_fixed.T)
+    ]
     return pl.pallas_call(
         kernel,
-        out_shape=jax.ShapeDtypeStruct((count, width + 2 * experts), jnp.bfloat16),
-        in_specs=[pl.BlockSpec(memory_space=pltpu.VMEM)] * 3,
+        out_shape=pltpu.VMEM((count, width + 2 * experts), jnp.bfloat16),
+        in_specs=[pl.BlockSpec(memory_space=pl.ANY)] * 3,
         out_specs=pl.BlockSpec(memory_space=pltpu.VMEM),
+        scratch_shapes=[pltpu.VMEM(value.shape, value.dtype) for value in given]
+        + [pltpu.SemaphoreType.DMA((3,))],
         compiler_params=pltpu.CompilerParams(vmem_limit_bytes=2 * 2**20),
         name="pack_tokens",
-    )(tokens, routes.T, gate_fixed.T)
+    )(*given)
 
 
 def fetched(weights):
-    pieces = 3
+    pieces = 6
 
     def kernel(*refs):
         number = len(weights)
@@ -138,55 +154,110 @@
     )(*placed)
 
 
-def expert_chunks(chunks, expert, w_gate, w_up, w_down, width):
+def expert_chunks(chunks, expert, weights, inside, width):
     count = chunks[0].shape[0]
     wide = chunks[0].shape[1]
     experts = (wide - width) // 2
     number = len(chunks)
     rows = number * count
+    half, quarter = rows // 2, rows // 4
+    units = weights[0].shape[0]
     tail = width // 128 * 128
     step = 768
+    pieces = 3
+    piece = units // pieces // 16 * 16
+    outside = [n for n in range(3) if not inside[n]]
 
     def kernel(*refs):
         expert_ref = refs[0]
         in_refs = refs[1 : 1 + number]
-        wg_ref, wu_ref, wd_ref = refs[1 + number : 4 + number]
-        out_refs = refs[4 + number : 4 + 2 * number]
-        x_ref = refs[4 + 2 * number]
+        w_refs = list(refs[1 + number : 4 + number])
+        kept_ref, far_ref, near_ref, x_ref, g_ref, h_ref = refs[4 + number : 10 + number]
+        spare, sem = refs[10 + number : -1], refs[-1]
+        copies = {}
+        for m, n in enumerate(outside):
+            copies[n] = []
+            for k in range(pieces):
+                span = pl.ds(k * piece, piece if k < pieces - 1 else units - k * piece)
+                copies[n].append(
+                    pltpu.make_async_copy(
+                        w_refs[n].at[span], spare[m].at[span], sem.at[m * pieces + k]
+                    )
+                )
+                copies[n][-1].start()
+            w_refs[n] = spare[m]
         for n in range(number):
             x_ref[n * count : (n + 1) * count, :] = in_refs[n][...]
-        lanes = lax.broadcasted_iota(jnp.int32, (8, wide - tail), 1) - (width - tail)
-        mine = (lanes == expert_ref[0]) | (lanes == expert_ref[0] + experts)
         nt = (((1,), (1,)), ((), ()))
-        share = lax.dot_general(
-            jnp.where(mine, 1.0, 0.0).astype(jnp.bfloat16),
-            x_ref[:, tail:],
-            nt,
-            preferred_element_type=jnp.float32,
-        )[0:1, :]
-        x = x_ref[:, :width]
-        gate = lax.dot_general(wg_ref[...], x, nt, preferred_element_type=jnp.float32)
-        up = lax.dot_general(wu_ref[...], x, nt, preferred_element_type=jnp.float32)
-        hidden = gate / (1.0 + jnp.exp(-gate)) * up * share
-        hidden = hidden.T.astype(jnp.bfloat16)
-        for start in range(0, width, step):
-            size = min(step, width - start)
-            part = jnp.dot(
-                hidden, wd_ref[:, start : start + size], preferred_element_type=jnp.float32
-            ).astype(jnp.bfloat16)
-            for m in range(number):
-                out_refs[m][:, start : start + size] = part[m * count : (m + 1) * count, :]
+
+        def ready(n):
+            for copy in copies.get(n, ()):
+                copy.wait()
+
+        @pl.when(expert_ref[0] >= 0)
+        def _():
+            ready(0)
+            g_ref[...] = lax.dot_general(
+                w_refs[0][...], x_ref[:, :width], nt, preferred_element_type=jnp.float32
+            )
+
+        @pl.when(expert_ref[0] >= 0)
+        def _():
+            ready(1)
+            lanes = lax.broadcasted_iota(jnp.int32, (8, wide - tail), 1) - (width - tail)
+            mine = (lanes == expert_ref[0]) | (lanes == expert_ref[0] + experts)
+            share = lax.dot_general(
+                jnp.where(mine, 1.0, 0.0).astype(jnp.bfloat16),
+                x_ref[:, tail:],
+                nt,
+                preferred_element_type=jnp.float32,
+            )[0:1, :]
+            up = lax.dot_general(
+                w_refs[1][...], x_ref[:, :width], nt, preferred_element_type=jnp.float32
+            )
+            gate = g_ref[...]
+            hidden = gate / (1.0 + jnp.exp(-gate)) * up * share
+            h_ref[...] = hidden.T.astype(jnp.bfloat16)
+
+        @pl.when(expert_ref[0] >= 0)
+        def _():
+            ready(2)
+            hidden = h_ref[...]
+            for start in range(0, width, step):
+                stop = min(start + step, width)
+                part = jnp.dot(
+                    hidden, w_refs[2][:, start:stop], preferred_element_type=jnp.float32
+                )
+                kept_ref[:, start:stop] = part[:half, :]
+                far_ref[:, start:stop] = part[half : half + quarter, :].astype(jnp.bfloat16)
+                near_ref[:, start:stop] = part[half + quarter :, :].astype(jnp.bfloat16)
 
     vmem = pl.BlockSpec(memory_space=pltpu.VMEM)
+    placed = [
+        weights[n] if inside[n] else pltpu.with_memory_space_constraint(weights[n], pltpu.HBM)
+        for n in range(3)
+    ]
     return pl.pallas_call(
         kernel,
-        out_shape=[jax.ShapeDtypeStruct((count, width), jnp.bfloat16)] * number,
-        in_specs=[pl.BlockSpec(memory_space=pltpu.SMEM)] + [vmem] * (number + 3),
-        out_specs=[vmem] * number,
-        scratch_shapes=[pltpu.VMEM((rows, wide), jnp.bfloat16)],
-        compiler_params=pltpu.CompilerParams(vmem_limit_bytes=16 * 2**20),
+        out_shape=[
+            pltpu.VMEM((half, width), jnp.float32),
+            pltpu.VMEM((quarter, width), jnp.bfloat16),
+            pltpu.VMEM((quarter, width), jnp.bfloat16),
+        ],
+        in_specs=[pl.BlockSpec(memory_space=pltpu.SMEM)]
+        + [vmem] * number
+        + [vmem if inside[n] else pl.BlockSpec(memory_space=pl.ANY) for n in range(3)],
+        out_specs=[vmem] * 3,
+        scratch_shapes=[
+            pltpu.VMEM((rows, wide), jnp.bfloat16),
+            pltpu.VMEM((units, rows), jnp.float32),
+            pltpu.VMEM((rows, units), jnp.bfloat16),
+        ]
+        + [pltpu.VMEM(weights[n].shape, weights[n].dtype) for n in outside]
+        + [pltpu.SemaphoreType.DMA((max(1, pieces * len(outside)),))],
+        compiler_params=pltpu.CompilerParams(vmem_limit_bytes=32 * 2**20),
         name="expert_chunks",
-    )(expert, *chunks, w_gate, w_up, w_down)
+    )(expert, *chunks, *placed)
 
 
 def added(*values):
@@ -194,6 +265,10 @@
     for value in values[1:]:
         total = total + value.astype(jnp.float32)
     return total.astype(jnp.bfloat16)
+
+
+def apart(*values):
+    return lax.optimization_barrier(values)
 
 
 def dense(tokens, routes, gate_fixed, gate_weight, up_weight, down_weight):
@@ -203,26 +278,67 @@
     expert = jnp.right_shift(lax.axis_index("ep").astype(jnp.int32), 1).reshape(1)
     tokens, expert = lax.optimization_barrier((tokens, expert))
     own = pack_tokens(tokens, routes, gate_fixed, devices_ep // 2)
-    near = [own] + [turned(own, "ep", k) for k in range(1, layers)]
-    far = [swapped(near[k], "ep", 1) for k in range(layers)]
-    mine = near + far
-    theirs = [swapped(mine[k], "ep", 0) for k in range(len(mine))]
-    w_gate, w_up, w_down = fetched([gate_weight[0].T, up_weight[0].T, down_weight[0]])
-    parts = expert_chunks(mine + theirs, expert, w_gate, w_up, w_down, width)
-    kept, given = parts[: len(mine)], parts[len(mine) :]
-    back = [swapped(given[k], "ep", 0) for k in range(len(given))]
-    far_sums = [added(kept[layers + k], back[layers + k]) for k in range(layers)]
-    from_far = [swapped(far_sums[k], "ep", 1) for k in range(layers)]
-    near_sums = [added(kept[k], back[k], from_far[k]) for k in range(layers)]
-    home = [turned(near_sums[k], "ep", -k) for k in range(1, layers)]
-    return added(kept[0], back[0], from_far[0], *home)
+    straight, groups = (1,), ((2,), (3,), (0,))
+    order = [k for group in groups for k in group] + list(straight)
+    near = [own] + [moved(own, "ep", 4 * k) for k in range(1, layers)]
+    far = [
+        moved(own, "ep", 4 * k + 2)
+        if k in straight
+        else moved(near[k], "ep", 2)
+        for k in range(layers)
+    ]
+    mine = [far[k] for k in order] + [near[k] for k in order]
+    theirs = [moved(mine[k], "ep", 1) for k in range(len(mine))]
+    weights = [gate_weight[0].T, up_weight[0].T, down_weight[0]]
+    inside = [False] * 3
+    found = fetched([weights[k] for k in (0,)])
+    for k, value in zip((0,), found):
+        weights[k], inside[k] = value, True
+    found = fetched([weights[k] for k in (1,)])
+    for k, value in zip((1,), found):
+        weights[k], inside[k] = value, True
+    kept, far_given, near_given = expert_chunks(
+        mine + theirs, expert, weights, inside, width
+    )
+    far_back = moved(far_given, "ep", 1)
+    near_back = moved(near_given, "ep", 1)
+    count = tokens.shape[0]
+    kept_near = kept[layers * count :]
+
+    def rows(start, stop):
+        return slice(start * count, stop * count)
+
+    from_far = {}
+    first = 0
+    for group in groups:
+        cut = rows(first, first + len(group))
+        value = added(*apart(kept[cut], far_back[cut]))
+        value = moved(value, "ep", 2)
+        for m, k in enumerate(group):
+            from_far[k] = value[rows(m, m + 1)]
+        first += len(group)
+    home = []
+    for n, k in enumerate(order):
+        cut = rows(n, n + 1)
+        if k in straight:
+            value = added(*apart(kept[cut], far_back[cut]))
+            home.append(moved(value, "ep", 4 * k + 2))
+            parts = apart(kept_near[cut], near_back[cut])
+        else:
+            parts = apart(kept_near[cut], near_back[cut], from_far[k])
+        if k:
+            value = added(*parts)
+            home.append(moved(value, "ep", 4 * k))
+        else:
+            home.extend(parts)
+    return added(*home)
 
 
 def local(tokens, routes, gate_fixed, gate_weight, up_weight, down_weight):
     devices_ep = lax.axis_size("ep")
     tok_count, top_count = routes.shape
     capacity = min(tok_count, 2 * tok_count * top_count // (devices_ep // 2))
-    if capacity == tok_count and devices_ep % 4 == 0:
+    if capacity == tok_count and devices_ep in (4, 8, 16, 32, 64):
         return dense(tokens, routes, gate_fixed, gate_weight, up_weight, down_weight)
     return slotted(tokens, routes, gate_fixed, gate_weight, up_weight, down_weight, capacity)
 

time: 57.4 us -> 52.9 us (0.922)
  waiting for transfers between devices: 25.6 us -> 18.9 us
  starting transfers between devices: 19.5 us -> 22.8 us
  local copies, waits for them, and re-layouts: 2.25 us -> 0.16 us
  Pallas kernels: 8.83 us -> 9.82 us
    ppermute x30 -> x24, waiting for transfers between devices: 25.6 us -> 18.9 us  [moved(): return lax.ppermute(value, axis, pairs)]
    ppermute x30 -> x24, starting transfers between devices: 19.5 us -> 22.8 us  [moved(): return lax.ppermute(value, axis, pairs)]
    unnamed x6 -> x0, local copies, waits for them, and re-layouts: 2.25 us -> none
    pallas_call x2, Pallas kernels: 4.09 us -> 5.35 us  [the longest x1 4.37 us: expert_chunks(): pl.pallas_call(kernel, out_shape=[pltpu.VMEM((half, width), jnp.float32),...]
    pallas_call x1 -> x2, Pallas kernels: 4.73 us -> 4.47 us  [fetched(): pl.pallas_call(kernel, out_shape=[pltpu.VMEM(weight.shape, weight.dtype)...]
  transfers between devices with their start and end apart: 30 -> 24, of which waited for: 11 -> 9; matrix products, arithmetic and copies ran while one was open for 0% -> 1% of each run, Pallas kernels for 8% -> 8%
where the time goes in v1:
time: 52.9 us; the launch traced here: 52.7 us
  starting transfers between devices  22.8 us (43%)
  waiting for transfers between devices  18.9 us (36%)
  Pallas kernels  9.82 us (19%)
  other arithmetic  0.92 us (2%)
    ppermute x24, starting transfers between devices, moved(): return lax.ppermute(value, axis, pairs)  22.8 us
    ppermute x24, waiting for transfers between devices, moved(): return lax.ppermute(value, axis, pairs)  18.9 us
    pallas_call x2, Pallas kernels, fetched(): pl.pallas_call(kernel, out_shape=[pltpu.VMEM(weight.shape, weight.dtype)...  4.47 us
    pallas_call x1, Pallas kernels, expert_chunks(): pl.pallas_call(kernel, out_shape=[pltpu.VMEM((half, width), jnp.float32),...  4.37 us
  transfers between devices with their start and end apart: 24, of which 9 were waited for; matrix products, arithmetic and copies ran while one was open for 1% of the time, Pallas kernels for 8%

profile of v1, /device:TPU:0, one launch (start us, length us, event | category | flops | bytes accessed | tf_op | source)
XLA Modules:
  0.0 52.7 jit_solution(9970128165388974150)
XLA Ops:
  0.0 1.0 %pack_tokens.1.refs_7_ = bf16[16,2896]{1,0:T(8,128)(2,1)S(1)} custom-call(bf16[16,2880]{1,0:T(8,128)(2,1)} %tok_hbm, s32[4,16]{1,0:T(4,128)} %bitcast.13, s32[4,16]{1,0:T(4,128)} %bitcast.14), custom_call_target="tpu_custom_call" | custom-call | tf_op jit(solution)/shard_map/pack_tokens/pallas_call | solution.py:110
  1.0 0.6 %collective-permute-start.13 = (bf16[16,2896]{1,0:T(8,128)(2,1)S(1)}, bf16[16,2896]{1,0:T(8,128)(2,1)S(1)}, u32[]{:S(2)}, u32[]{:S(2)}) collective-permute-start(bf16[16,2896]{1,0:T(8,128)(2,1)S(1)} %pack_tokens.1.refs_7_), channel_id=1, source_target_pairs={{0,1},{1,0},{2,3},{3,2},{4,5},{5,4},{6,7},{7,6},{8,9},{9,8},{10,11... | collective-permute-start | bytes 278024 | tf_op jit(solution)/shard_map/ppermute | solution.py:17
  1.6 2.6 %collective-permute-start.6 = (bf16[16,2896]{1,0:T(8,128)(2,1)S(1)}, bf16[16,2896]{1,0:T(8,128)(2,1)S(1)}, u32[]{:S(2)}, u32[]{:S(2)}) collective-permute-start(bf16[16,2896]{1,0:T(8,128)(2,1)S(1)} %pack_tokens.1.refs_7_), channel_id=1, source_target_pairs={{0,4},{1,5},{2,6},{3,7},{4,0},{5,1},{6,2},{7,3},{8,12},{9,13},{10,... | collective-permute-start | bytes 278024 | tf_op jit(solution)/shard_map/ppermute | solution.py:17
  4.2 1.4 %collective-permute-start.5 = (bf16[16,2896]{1,0:T(8,128)(2,1)S(1)}, bf16[16,2896]{1,0:T(8,128)(2,1)S(1)}, u32[]{:S(2)}, u32[]{:S(2)}) collective-permute-start(bf16[16,2896]{1,0:T(8,128)(2,1)S(1)} %pack_tokens.1.refs_7_), channel_id=1, source_target_pairs={{0,6},{1,7},{2,4},{3,5},{4,2},{5,3},{6,0},{7,1},{8,14},{9,15},{10,... | collective-permute-start | bytes 278024 | tf_op jit(solution)/shard_map/ppermute | solution.py:17
  5.6 3.6 %collective-permute-start.2 = (bf16[16,2896]{1,0:T(8,128)(2,1)S(1)}, bf16[16,2896]{1,0:T(8,128)(2,1)S(1)}, u32[]{:S(2)}, u32[]{:S(2)}) collective-permute-start(bf16[16,2896]{1,0:T(8,128)(2,1)S(1)} %pack_tokens.1.refs_7_), channel_id=1, source_target_pairs={{0,12},{1,13},{2,14},{3,15},{4,8},{5,9},{6,10},{7,11},{8,4},{9,5},... | collective-permute-start | bytes 278024 | tf_op jit(solution)/shard_map/ppermute | solution.py:17
  9.2 0.0 collective-permute-start
  9.2 0.0 collective-permute-done.13.refs_15_
  9.2 0.5 %collective-permute-start.4 = (bf16[16,2896]{1,0:T(8,128)(2,1)S(1)}, bf16[16,2896]{1,0:T(8,128)(2,1)S(1)}, u32[]{:S(2)}, u32[]{:S(2)}) collective-permute-start(bf16[16,2896]{1,0:T(8,128)(2,1)S(1)} %pack_tokens.1.refs_7_), channel_id=1, source_target_pairs={{0,2},{1,3},{2,0},{3,1},{4,6},{5,7},{6,4},{7,5},{8,10},{9,11},{10,... | collective-permute-start | bytes 278024 | tf_op jit(solution)/shard_map/ppermute | solution.py:17
  9.7 0.0 collective-permute-done.6.refs_8_
  9.7 0.9 %collective-permute-done.5.refs_4_ = bf16[16,2896]{1,0:T(8,128)(2,1)S(1)} collective-permute-done((bf16[16,2896]{1,0:T(8,128)(2,1)S(1)}, bf16[16,2896]{1,0:T(8,128)(2,1)S(1)}, u32[]{:S(2)}, u32[]{:S(2)}) %collective-permute-start.5) | collective-permute-done | bytes 92704 | tf_op jit(solution)/shard_map/ppermute | solution.py:17
  10.6 4.2 %collective-permute-done.2.refs_6_ = bf16[16,2896]{1,0:T(8,128)(2,1)S(1)} collective-permute-done((bf16[16,2896]{1,0:T(8,128)(2,1)S(1)}, bf16[16,2896]{1,0:T(8,128)(2,1)S(1)}, u32[]{:S(2)}, u32[]{:S(2)}) %collective-permute-start.2) | collective-permute-done | bytes 92704 | tf_op jit(solution)/shard_map/ppermute | solution.py:17
  14.8 1.0 %collective-permute-start.3 = (bf16[16,2896]{1,0:T(8,128)(2,1)S(1)}, bf16[16,2896]{1,0:T(8,128)(2,1)S(1)}, u32[]{:S(2)}, u32[]{:S(2)}) collective-permute-start(bf16[16,2896]{1,0:T(8,128)(2,1)S(1)} %collective-permute-done.2.refs_6_), channel_id=1, source_target_pairs={{0,2},{1,3},{2,0},{3,1},{4,6},{5,7},{6,4},{7,5},{8,10},{9,11},{10,... | collective-permute-start | bytes 278024 | tf_op jit(solution)/shard_map/ppermute | solution.py:17
  15.9 1.9 %collective-permute-done.refs_5_ = bf16[16,2896]{1,0:T(8,128)(2,1)S(1)} collective-permute-done((bf16[16,2896]{1,0:T(8,128)(2,1)S(1)}, bf16[16,2896]{1,0:T(8,128)(2,1)S(1)}, u32[]{:S(2)}, u32[]{:S(2)}) %collective-permute-start) | collective-permute-done | bytes 92704 | tf_op jit(solution)/shard_map/ppermute | solution.py:17
  17.7 1.0 %collective-permute-start.1 = (bf16[16,2896]{1,0:T(8,128)(2,1)S(1)}, bf16[16,2896]{1,0:T(8,128)(2,1)S(1)}, u32[]{:S(2)}, u32[]{:S(2)}) collective-permute-start(bf16[16,2896]{1,0:T(8,128)(2,1)S(1)} %collective-permute-done.refs_5_), channel_id=1, source_target_pairs={{0,2},{1,3},{2,0},{3,1},{4,6},{5,7},{6,4},{7,5},{8,10},{9,11},{10,... | collective-permute-start | bytes 278024 | tf_op jit(solution)/shard_map/ppermute | solution.py:17
  18.8 0.0 collective-permute-done.4.refs_3_
  18.8 0.0 collective-permute-start.12
  18.8 0.0 collective-permute-done.14.refs_16_
  18.8 0.5 collective-permute-start.11
  19.3 0.0 collective-permute-done.10.refs_12_
  19.3 0.1 collective-permute-start.9
  19.4 0.0 collective-permute-done.3.refs_2_
  19.4 0.4 collective-permute-start.8
  19.8 2.5 %collective-permute-done.1.refs_1_ = bf16[16,2896]{1,0:T(8,128)(2,1)S(1)} collective-permute-done((bf16[16,2896]{1,0:T(8,128)(2,1)S(1)}, bf16[16,2896]{1,0:T(8,128)(2,1)S(1)}, u32[]{:S(2)}, u32[]{:S(2)}) %collective-permute-start.1) | collective-permute-done | bytes 92704 | tf_op jit(solution)/shard_map/ppermute | solution.py:17
  22.3 0.0 collective-permute-start.7
  22.3 2.2 %fetch.2.refs_17_ = bf16[720,2880]{1,0:T(8,128)(2,1)S(1)} custom-call(bf16[720,2880]{1,0:T(8,128)(2,1)} %bitcast.11), custom_call_target="tpu_custom_call" | custom-call | tf_op jit(solution)/shard_map/fetch/pallas_call | solution.py:146
  24.5 2.2 %fetch.3.refs_18_ = bf16[720,2880]{1,0:T(8,128)(2,1)S(1)} custom-call(bf16[720,2880]{1,0:T(8,128)(2,1)} %bitcast.12), custom_call_target="tpu_custom_call" | custom-call | tf_op jit(solution)/shard_map/fetch/pallas_call | solution.py:146
  26.8 0.0 collective-permute-done.9.refs_11_
  26.8 0.0 collective-permute-done.11.refs_13_
  26.8 0.0 collective-permute-done.8.refs_10_
  26.8 4.4 %expert_chunks.1 = (f32[128,2880]{1,0:T(8,128)S(1)}, bf16[64,2880]{1,0:T(8,128)(2,1)S(1)}, bf16[64,2880]{1,0:T(8,128)(2,1)S(1)}) custom-call(s32[1]{0:T(128)} %bitcast.refs_0_, bf16[16,2896]{1,0:T(8,128)(2,1)S(1)} %collective-permute-done.1.refs_1_, bf16[16,2896]{1,0:T(8,128)(2,1)S(1)} %collective-permute-done.3.refs_2_, ...), custom_call_target="tpu_custom_call" | custom-call | tf_op jit(solution)/shard_map/expert_chunks/pallas_call | solution.py:240
  31.2 0.6 %collective-permute-start.15 = (bf16[64,2880]{1,0:T(8,128)(2,1)S(1)}, bf16[64,2880]{1,0:T(8,128)(2,1)S(1)}, u32[]{:S(2)}, u32[]{:S(2)}) collective-permute-start(bf16[64,2880]{1,0:T(8,128)(2,1)S(1)} %get-tuple-element.32), channel_id=1, source_target_pairs={{0,1},{1,0},{2,3},{3,2},{4,5},{5,4},{6,7},{7,6},{8,9},{9,8},{10,11... | collective-permute-start | bytes 1105928 | tf_op jit(solution)/shard_map/ppermute | solution.py:17
  31.8 0.1 collective-permute-start.16
  31.9 0.1 fusion
  32.0 1.1 %collective-permute-done.15 = bf16[64,2880]{1,0:T(8,128)(2,1)S(1)} collective-permute-done((bf16[64,2880]{1,0:T(8,128)(2,1)S(1)}, bf16[64,2880]{1,0:T(8,128)(2,1)S(1)}, u32[]{:S(2)}, u32[]{:S(2)}) %collective-permute-start.15) | collective-permute-done | bytes 368672 | tf_op jit(solution)/shard_map/ppermute | solution.py:17
  33.2 0.1 collective-permute-start.23
  33.3 0.4 collective-permute-done.16
  33.7 1.1 %collective-permute-start.19 = (bf16[16,2880]{1,0:T(8,128)(2,1)S(1)}, bf16[16,2880]{1,0:T(8,128)(2,1)S(1)}, u32[]{:S(2)}, u32[]{:S(2)}) collective-permute-start(bf16[16,2880]{1,0:T(8,128)(2,1)S(1)} %add_convert_fusion.5), channel_id=1, source_target_pairs={{0,2},{1,3},{2,0},{3,1},{4,6},{5,7},{6,4},{7,5},{8,10},{9,11},{10,... | collective-permute-start | bytes 276488 | tf_op jit(solution)/shard_map/ppermute | solution.py:17
  34.9 1.0 %collective-permute-start.21 = (bf16[16,2880]{1,0:T(8,128)(2,1)S(1)}, bf16[16,2880]{1,0:T(8,128)(2,1)S(1)}, u32[]{:S(2)}, u32[]{:S(2)}) collective-permute-start(bf16[16,2880]{1,0:T(8,128)(2,1)S(1)} %add_convert_fusion.3), channel_id=1, source_target_pairs={{0,2},{1,3},{2,0},{3,1},{4,6},{5,7},{6,4},{7,5},{8,10},{9,11},{10,... | collective-permute-start | bytes 276488 | tf_op jit(solution)/shard_map/ppermute | solution.py:17
  35.9 2.2 %collective-permute-start.22 = (bf16[16,2880]{1,0:T(8,128)(2,1)S(1)}, bf16[16,2880]{1,0:T(8,128)(2,1)S(1)}, u32[]{:S(2)}, u32[]{:S(2)}) collective-permute-start(bf16[16,2880]{1,0:T(8,128)(2,1)S(1)} %add_convert_fusion.2), channel_id=1, source_target_pairs={{0,6},{1,7},{2,4},{3,5},{4,2},{5,3},{6,0},{7,1},{8,14},{9,15},{10,... | collective-permute-start | bytes 276488 | tf_op jit(solution)/shard_map/ppermute | solution.py:17
  38.1 1.0 %collective-permute-start.17 = (bf16[16,2880]{1,0:T(8,128)(2,1)S(1)}, bf16[16,2880]{1,0:T(8,128)(2,1)S(1)}, u32[]{:S(2)}, u32[]{:S(2)}) collective-permute-start(bf16[16,2880]{1,0:T(8,128)(2,1)S(1)} %add_convert_fusion.7), channel_id=1, source_target_pairs={{0,2},{1,3},{2,0},{3,1},{4,6},{5,7},{6,4},{7,5},{8,10},{9,11},{10,... | collective-permute-start | bytes 276488 | tf_op jit(solution)/shard_map/ppermute | solution.py:17
  39.2 0.2 collective-permute-done.19
  39.4 3.1 %collective-permute-start.20 = (bf16[16,2880]{1,0:T(8,128)(2,1)S(1)}, bf16[16,2880]{1,0:T(8,128)(2,1)S(1)}, u32[]{:S(2)}, u32[]{:S(2)}) collective-permute-start(bf16[16,2880]{1,0:T(8,128)(2,1)S(1)} %add_convert_fusion.4), channel_id=1, source_target_pairs={{0,12},{1,13},{2,14},{3,15},{4,8},{5,9},{6,10},{7,11},{8,4},{9,5},... | collective-permute-start | bytes 276488 | tf_op jit(solution)/shard_map/ppermute | solution.py:17
  42.5 2.3 %collective-permute-done.17 = bf16[16,2880]{1,0:T(8,128)(2,1)S(1)} collective-permute-done((bf16[16,2880]{1,0:T(8,128)(2,1)S(1)}, bf16[16,2880]{1,0:T(8,128)(2,1)S(1)}, u32[]{:S(2)}, u32[]{:S(2)}) %collective-permute-start.17) | collective-permute-done | bytes 92192 | tf_op jit(solution)/shard_map/ppermute | solution.py:17
  44.9 1.8 %collective-permute-start.18 = (bf16[16,2880]{1,0:T(8,128)(2,1)S(1)}, bf16[16,2880]{1,0:T(8,128)(2,1)S(1)}, u32[]{:S(2)}, u32[]{:S(2)}) collective-permute-start(bf16[16,2880]{1,0:T(8,128)(2,1)S(1)} %add_convert_fusion.6), channel_id=1, source_target_pairs={{0,8},{1,9},{2,10},{3,11},{4,12},{5,13},{6,14},{7,15},{8,0},{9,1},... | collective-permute-start | bytes 276488 | tf_op jit(solution)/shard_map/ppermute | solution.py:17
  46.7 0.0 collective-permute-done.21
  46.7 0.0 collective-permute-done.23
  46.7 5.3 %collective-permute-done.18 = bf16[16,2880]{1,0:T(8,128)(2,1)S(1)} collective-permute-done((bf16[16,2880]{1,0:T(8,128)(2,1)S(1)}, bf16[16,2880]{1,0:T(8,128)(2,1)S(1)}, u32[]{:S(2)}, u32[]{:S(2)}) %collective-permute-start.18) | collective-permute-done | bytes 92192 | tf_op jit(solution)/shard_map/ppermute | solution.py:17
  52.0 0.7 %add_convert_fusion = bf16[16,2880]{1,0:T(8,128)(2,1)} fusion(bf16[16,2880]{1,0:T(8,128)(2,1)S(1)} %collective-permute-done.23, bf16[16,2880]{1,0:T(8,128)(2,1)S(1)} %collective-permute-done.22, bf16[16,2880]{1,0:T(8,128)(2,1)S(1)} %collective-permute-done.21, bf16[16,2880]{1,0:T(8,128)(2,1)S(1)} %get-tuple-element.47, f32[16,2880]{1,0:T(8,128)S(1)} %get-tuple-element.46, ...), kind=kLoop, calls=%fused_computation | loop fusion | flops 599040 | bytes 829440 | tf_op jit(solution)/shard_map/convert_element_type | solution.py:267
  (15 shorter events, 0.3 us)
Async XLA Ops:
  1.0 8.2 %collective-permute-start.13 = (bf16[16,2896]{1,0:T(8,128)(2,1)S(1)}, bf16[16,2896]{1,0:T(8,128)(2,1)S(1)}, u32[]{:S(2)}, u32[]{:S(2)}) collective-permute-start(bf16[16,2896]{1,0:T(8,128)(2,1)S(1)} %pack_tokens.1.refs_7_), channel_id=1, source_target_pairs={{0,1},{1,0},{2,3},{3,2},{4,5},{5,4},{6,7},{7,6},{8,9},{9,8},{10,11... | collective-permute-start | bytes 278024 | tf_op jit(solution)/shard_map/ppermute | solution.py:17
  1.6 8.2 %collective-permute-start.6 = (bf16[16,2896]{1,0:T(8,128)(2,1)S(1)}, bf16[16,2896]{1,0:T(8,128)(2,1)S(1)}, u32[]{:S(2)}, u32[]{:S(2)}) collective-permute-start(bf16[16,2896]{1,0:T(8,128)(2,1)S(1)} %pack_tokens.1.refs_7_), channel_id=1, source_target_pairs={{0,4},{1,5},{2,6},{3,7},{4,0},{5,1},{6,2},{7,3},{8,12},{9,13},{10,... | collective-permute-start | bytes 278024 | tf_op jit(solution)/shard_map/ppermute | solution.py:17
  4.2 6.4 %collective-permute-start.5 = (bf16[16,2896]{1,0:T(8,128)(2,1)S(1)}, bf16[16,2896]{1,0:T(8,128)(2,1)S(1)}, u32[]{:S(2)}, u32[]{:S(2)}) collective-permute-start(bf16[16,2896]{1,0:T(8,128)(2,1)S(1)} %pack_tokens.1.refs_7_), channel_id=1, source_target_pairs={{0,6},{1,7},{2,4},{3,5},{4,2},{5,3},{6,0},{7,1},{8,14},{9,15},{10,... | collective-permute-start | bytes 278024 | tf_op jit(solution)/shard_map/ppermute | solution.py:17
  5.6 9.3 %collective-permute-start.2 = (bf16[16,2896]{1,0:T(8,128)(2,1)S(1)}, bf16[16,2896]{1,0:T(8,128)(2,1)S(1)}, u32[]{:S(2)}, u32[]{:S(2)}) collective-permute-start(bf16[16,2896]{1,0:T(8,128)(2,1)S(1)} %pack_tokens.1.refs_7_), channel_id=1, source_target_pairs={{0,12},{1,13},{2,14},{3,15},{4,8},{5,9},{6,10},{7,11},{8,4},{9,5},... | collective-permute-start | bytes 278024 | tf_op jit(solution)/shard_map/ppermute | solution.py:17
  9.2 8.6 %collective-permute-start = (bf16[16,2896]{1,0:T(8,128)(2,1)S(1)}, bf16[16,2896]{1,0:T(8,128)(2,1)S(1)}, u32[]{:S(2)}, u32[]{:S(2)}) collective-permute-start(bf16[16,2896]{1,0:T(8,128)(2,1)S(1)} %pack_tokens.1.refs_7_), channel_id=1, source_target_pairs={{0,8},{1,9},{2,10},{3,11},{4,12},{5,13},{6,14},{7,15},{8,0},{9,1},... | collective-permute-start | bytes 278024 | tf_op jit(solution)/shard_map/ppermute | solution.py:17
  9.2 9.6 %collective-permute-start.4 = (bf16[16,2896]{1,0:T(8,128)(2,1)S(1)}, bf16[16,2896]{1,0:T(8,128)(2,1)S(1)}, u32[]{:S(2)}, u32[]{:S(2)}) collective-permute-start(bf16[16,2896]{1,0:T(8,128)(2,1)S(1)} %pack_tokens.1.refs_7_), channel_id=1, source_target_pairs={{0,2},{1,3},{2,0},{3,1},{4,6},{5,7},{6,4},{7,5},{8,10},{9,11},{10,... | collective-permute-start | bytes 278024 | tf_op jit(solution)/shard_map/ppermute | solution.py:17
  9.7 9.1 %collective-permute-start.14 = (bf16[16,2896]{1,0:T(8,128)(2,1)S(1)}, bf16[16,2896]{1,0:T(8,128)(2,1)S(1)}, u32[]{:S(2)}, u32[]{:S(2)}) collective-permute-start(bf16[16,2896]{1,0:T(8,128)(2,1)S(1)} %collective-permute-done.6.refs_8_), channel_id=1, source_target_pairs={{0,1},{1,0},{2,3},{3,2},{4,5},{5,4},{6,7},{7,6},{8,9},{9,8},{10,11... | collective-permute-start | bytes 278024 | tf_op jit(solution)/shard_map/ppermute | solution.py:17
  10.6 8.7 %collective-permute-start.10 = (bf16[16,2896]{1,0:T(8,128)(2,1)S(1)}, bf16[16,2896]{1,0:T(8,128)(2,1)S(1)}, u32[]{:S(2)}, u32[]{:S(2)}) collective-permute-start(bf16[16,2896]{1,0:T(8,128)(2,1)S(1)} %collective-permute-done.5.refs_4_), channel_id=1, source_target_pairs={{0,1},{1,0},{2,3},{3,2},{4,5},{5,4},{6,7},{7,6},{8,9},{9,8},{10,11... | collective-permute-start | bytes 278024 | tf_op jit(solution)/shard_map/ppermute | solution.py:17
  14.8 4.6 %collective-permute-start.3 = (bf16[16,2896]{1,0:T(8,128)(2,1)S(1)}, bf16[16,2896]{1,0:T(8,128)(2,1)S(1)}, u32[]{:S(2)}, u32[]{:S(2)}) collective-permute-start(bf16[16,2896]{1,0:T(8,128)(2,1)S(1)} %collective-permute-done.2.refs_6_), channel_id=1, source_target_pairs={{0,2},{1,3},{2,0},{3,1},{4,6},{5,7},{6,4},{7,5},{8,10},{9,11},{10,... | collective-permute-start | bytes 278024 | tf_op jit(solution)/shard_map/ppermute | solution.py:17
  17.7 4.6 %collective-permute-start.1 = (bf16[16,2896]{1,0:T(8,128)(2,1)S(1)}, bf16[16,2896]{1,0:T(8,128)(2,1)S(1)}, u32[]{:S(2)}, u32[]{:S(2)}) collective-permute-start(bf16[16,2896]{1,0:T(8,128)(2,1)S(1)} %collective-permute-done.refs_5_), channel_id=1, source_target_pairs={{0,2},{1,3},{2,0},{3,1},{4,6},{5,7},{6,4},{7,5},{8,10},{9,11},{10,... | collective-permute-start | bytes 278024 | tf_op jit(solution)/shard_map/ppermute | solution.py:17
  18.8 8.0 %collective-permute-start.12 = (bf16[16,2896]{1,0:T(8,128)(2,1)S(1)}, bf16[16,2896]{1,0:T(8,128)(2,1)S(1)}, u32[]{:S(2)}, u32[]{:S(2)}) collective-permute-start(bf16[16,2896]{1,0:T(8,128)(2,1)S(1)} %collective-permute-done.2.refs_6_), channel_id=1, source_target_pairs={{0,1},{1,0},{2,3},{3,2},{4,5},{5,4},{6,7},{7,6},{8,9},{9,8},{10,11... | collective-permute-start | bytes 278024 | tf_op jit(solution)/shard_map/ppermute | solution.py:17
  18.8 8.0 %collective-permute-start.11 = (bf16[16,2896]{1,0:T(8,128)(2,1)S(1)}, bf16[16,2896]{1,0:T(8,128)(2,1)S(1)}, u32[]{:S(2)}, u32[]{:S(2)}) collective-permute-start(bf16[16,2896]{1,0:T(8,128)(2,1)S(1)} %collective-permute-done.refs_5_), channel_id=1, source_target_pairs={{0,1},{1,0},{2,3},{3,2},{4,5},{5,4},{6,7},{7,6},{8,9},{9,8},{10,11... | collective-permute-start | bytes 278024 | tf_op jit(solution)/shard_map/ppermute | solution.py:17
  19.3 7.5 %collective-permute-start.9 = (bf16[16,2896]{1,0:T(8,128)(2,1)S(1)}, bf16[16,2896]{1,0:T(8,128)(2,1)S(1)}, u32[]{:S(2)}, u32[]{:S(2)}) collective-permute-start(bf16[16,2896]{1,0:T(8,128)(2,1)S(1)} %collective-permute-done.4.refs_3_), channel_id=1, source_target_pairs={{0,1},{1,0},{2,3},{3,2},{4,5},{5,4},{6,7},{7,6},{8,9},{9,8},{10,11... | collective-permute-start | bytes 278024 | tf_op jit(solution)/shard_map/ppermute | solution.py:17
  19.4 7.4 %collective-permute-start.8 = (bf16[16,2896]{1,0:T(8,128)(2,1)S(1)}, bf16[16,2896]{1,0:T(8,128)(2,1)S(1)}, u32[]{:S(2)}, u32[]{:S(2)}) collective-permute-start(bf16[16,2896]{1,0:T(8,128)(2,1)S(1)} %collective-permute-done.3.refs_2_), channel_id=1, source_target_pairs={{0,1},{1,0},{2,3},{3,2},{4,5},{5,4},{6,7},{7,6},{8,9},{9,8},{10,11... | collective-permute-start | bytes 278024 | tf_op jit(solution)/shard_map/ppermute | solution.py:17
  22.3 4.5 %collective-permute-start.7 = (bf16[16,2896]{1,0:T(8,128)(2,1)S(1)}, bf16[16,2896]{1,0:T(8,128)(2,1)S(1)}, u32[]{:S(2)}, u32[]{:S(2)}) collective-permute-start(bf16[16,2896]{1,0:T(8,128)(2,1)S(1)} %collective-permute-done.1.refs_1_), channel_id=1, source_target_pairs={{0,1},{1,0},{2,3},{3,2},{4,5},{5,4},{6,7},{7,6},{8,9},{9,8},{10,11... | collective-permute-start | bytes 278024 | tf_op jit(solution)/shard_map/ppermute | solution.py:17
  31.2 1.9 %collective-permute-start.15 = (bf16[64,2880]{1,0:T(8,128)(2,1)S(1)}, bf16[64,2880]{1,0:T(8,128)(2,1)S(1)}, u32[]{:S(2)}, u32[]{:S(2)}) collective-permute-start(bf16[64,2880]{1,0:T(8,128)(2,1)S(1)} %get-tuple-element.32), channel_id=1, source_target_pairs={{0,1},{1,0},{2,3},{3,2},{4,5},{5,4},{6,7},{7,6},{8,9},{9,8},{10,11... | collective-permute-start | bytes 1105928 | tf_op jit(solution)/shard_map/ppermute | solution.py:17
  31.8 1.9 %collective-permute-start.16 = (bf16[64,2880]{1,0:T(8,128)(2,1)S(1)}, bf16[64,2880]{1,0:T(8,128)(2,1)S(1)}, u32[]{:S(2)}, u32[]{:S(2)}) collective-permute-start(bf16[64,2880]{1,0:T(8,128)(2,1)S(1)} %get-tuple-element.33), channel_id=1, source_target_pairs={{0,1},{1,0},{2,3},{3,2},{4,5},{5,4},{6,7},{7,6},{8,9},{9,8},{10,11... | collective-permute-start | bytes 1105928 | tf_op jit(solution)/shard_map/ppermute | solution.py:17
  33.2 13.5 %collective-permute-start.23 = (bf16[16,2880]{1,0:T(8,128)(2,1)S(1)}, bf16[16,2880]{1,0:T(8,128)(2,1)S(1)}, u32[]{:S(2)}, u32[]{:S(2)}) collective-permute-start(bf16[16,2880]{1,0:T(8,128)(2,1)S(1)} %add_convert_fusion.1), channel_id=1, source_target_pairs={{0,4},{1,5},{2,6},{3,7},{4,0},{5,1},{6,2},{7,3},{8,12},{9,13},{10,... | collective-permute-start | bytes 276488 | tf_op jit(solution)/shard_map/ppermute | solution.py:17
  33.7 5.7 %collective-permute-start.19 = (bf16[16,2880]{1,0:T(8,128)(2,1)S(1)}, bf16[16,2880]{1,0:T(8,128)(2,1)S(1)}, u32[]{:S(2)}, u32[]{:S(2)}) collective-permute-start(bf16[16,2880]{1,0:T(8,128)(2,1)S(1)} %add_convert_fusion.5), channel_id=1, source_target_pairs={{0,2},{1,3},{2,0},{3,1},{4,6},{5,7},{6,4},{7,5},{8,10},{9,11},{10,... | collective-permute-start | bytes 276488 | tf_op jit(solution)/shard_map/ppermute | solution.py:17
  34.9 11.8 %collective-permute-start.21 = (bf16[16,2880]{1,0:T(8,128)(2,1)S(1)}, bf16[16,2880]{1,0:T(8,128)(2,1)S(1)}, u32[]{:S(2)}, u32[]{:S(2)}) collective-permute-start(bf16[16,2880]{1,0:T(8,128)(2,1)S(1)} %add_convert_fusion.3), channel_id=1, source_target_pairs={{0,2},{1,3},{2,0},{3,1},{4,6},{5,7},{6,4},{7,5},{8,10},{9,11},{10,... | collective-permute-start | bytes 276488 | tf_op jit(solution)/shard_map/ppermute | solution.py:17
  35.9 10.8 %collective-permute-start.22 = (bf16[16,2880]{1,0:T(8,128)(2,1)S(1)}, bf16[16,2880]{1,0:T(8,128)(2,1)S(1)}, u32[]{:S(2)}, u32[]{:S(2)}) collective-permute-start(bf16[16,2880]{1,0:T(8,128)(2,1)S(1)} %add_convert_fusion.2), channel_id=1, source_target_pairs={{0,6},{1,7},{2,4},{3,5},{4,2},{5,3},{6,0},{7,1},{8,14},{9,15},{10,... | collective-permute-start | bytes 276488 | tf_op jit(solution)/shard_map/ppermute | solution.py:17
  38.1 6.7 %collective-permute-start.17 = (bf16[16,2880]{1,0:T(8,128)(2,1)S(1)}, bf16[16,2880]{1,0:T(8,128)(2,1)S(1)}, u32[]{:S(2)}, u32[]{:S(2)}) collective-permute-start(bf16[16,2880]{1,0:T(8,128)(2,1)S(1)} %add_convert_fusion.7), channel_id=1, source_target_pairs={{0,2},{1,3},{2,0},{3,1},{4,6},{5,7},{6,4},{7,5},{8,10},{9,11},{10,... | collective-permute-start | bytes 276488 | tf_op jit(solution)/shard_map/ppermute | solution.py:17
  39.4 7.3 %collective-permute-start.20 = (bf16[16,2880]{1,0:T(8,128)(2,1)S(1)}, bf16[16,2880]{1,0:T(8,128)(2,1)S(1)}, u32[]{:S(2)}, u32[]{:S(2)}) collective-permute-start(bf16[16,2880]{1,0:T(8,128)(2,1)S(1)} %add_convert_fusion.4), channel_id=1, source_target_pairs={{0,12},{1,13},{2,14},{3,15},{4,8},{5,9},{6,10},{7,11},{8,4},{9,5},... | collective-permute-start | bytes 276488 | tf_op jit(solution)/shard_map/ppermute | solution.py:17
  44.9 7.1 %collective-permute-start.18 = (bf16[16,2880]{1,0:T(8,128)(2,1)S(1)}, bf16[16,2880]{1,0:T(8,128)(2,1)S(1)}, u32[]{:S(2)}, u32[]{:S(2)}) collective-permute-start(bf16[16,2880]{1,0:T(8,128)(2,1)S(1)} %add_convert_fusion.6), channel_id=1, source_target_pairs={{0,8},{1,9},{2,10},{3,11},{4,12},{5,13},{6,14},{7,15},{8,0},{9,1},... | collective-permute-start | bytes 276488 | tf_op jit(solution)/shard_map/ppermute | solution.py:17
